TPU v7x, 128 devices: a whole 4x4x4 slice. The times are simulated.
128 devices in a mesh: seq: 16 (over x, z), head: 8 (over y, core).
Axes of the slice: x: 4, y: 4, z: 4, core: 2. Of those that a mesh axis runs over, the one named last changes fastest.
Arguments:
- queries: bfloat16 [16384, 8192], P('seq', 'head'), may hold values from -0.5390625 to 0.5390625
- keys: bfloat16 [16384, 8192], P('seq', 'head'), may hold values from -0.5390625 to 0.5390625
- values: bfloat16 [16384, 8192], P('seq', 'head'), may hold values from -6 to 6
- log_decay: float32 [16384, 64], P('seq', 'head'), may hold values from -1 to 0
- gain: float32 [8192], P('head'), may hold values from 0.1 to 1.9
- lengths: int32 [8], replicated, may hold values from 1 to 4096, 16384 in all
- out_grad: bfloat16 [16384, 8192], P('seq', 'head'), may hold values from -6 to 6
Outputs:
- normed: bfloat16 [16384, 8192], P('seq', 'head')
- grad_query: bfloat16 [16384, 8192], P('seq', 'head')
- grad_key: bfloat16 [16384, 8192], P('seq', 'head')
- grad_value: bfloat16 [16384, 8192], P('seq', 'head')
Inputs may be any that keep to these rules, and one draw needn't show every extreme that they name: The 8 lengths sum to 16384.
All inputs are finite; a program needn't handle non-finite values.
Results may differ from a plain program's by a relative error of at most 0.012.
Values sent between devices are 32-bit elements; how exact they have to be, the bound alone decides.
A program may use at most 128 MiB of HBM per device.

v0:
```python
import functools

import jax
import jax.numpy as jnp
from jax import lax
from jax.experimental import pallas as pl
from jax.experimental.pallas import tpu as pltpu
from jax.sharding import Mesh
from jax.sharding import PartitionSpec as P

BLOCK = 128
SEQ = ("x", "z")
MESH = pl.DeviceIdType.MESH
F32 = jnp.float32
BF16 = jnp.bfloat16
epsilon = 1e-06
MASKED = -1e30
SLAB = 2 * BLOCK + 8


def dot(left, right, left_axis=1, right_axis=0):
    dims = (((left_axis,), (right_axis,)), ((), ()))
    return lax.dot_general(left, right, dims, preferred_element_type=F32)


def rows_of(block):
    return pl.ds(pl.multiple_of(block * BLOCK, BLOCK), BLOCK)


def lanes_of(head):
    return slice(head * BLOCK, (head + 1) * BLOCK)


def as_columns(row):
    return jnp.transpose(jnp.broadcast_to(row, (BLOCK, BLOCK)))


def place(linear, head):
    linear = lax.rem(linear + 32, 16)
    return (lax.div(linear, 4), lax.rem(linear, 4), head)


class Exchange:
    def __init__(self, step, own, first_in, totals, near_in, far_in, back, result, send, recv):
        self.own, self.first_in, self.totals, self.near_in = own, first_in, totals, near_in
        self.far_in, self.back, self.result = far_in, back, result
        x, z, head = lax.axis_index("x"), lax.axis_index("z"), lax.axis_index("head")
        me = x * 4 + z
        odd = lax.rem(z, 2)
        outer = jnp.where((z == 0) | (z == 3), 0, 1)
        lower = jnp.where(z < 2, 2, 3)
        self.mine = (outer, lower)
        self.other = (1 - outer, 5 - lower)
        second = (odd == 1, odd == 0)
        self.lead = second if step == 1 else (odd == 0, odd == 1)
        partner = (me + 1 - 2 * odd, me - 1 + 2 * odd)
        near = [me + step * jnp.where(lead, 1, 3) for lead in self.lead]
        far = me + 4 * step

        def copy(source, target, index, linear):
            return pltpu.make_async_remote_copy(
                src_ref=source,
                dst_ref=target,
                send_sem=send.at[index],
                recv_sem=recv.at[index],
                device_id=place(linear, head),
                device_id_type=MESH,
            )

        self.one, self.near, self.far, self.three = [], [], [], []
        for i in range(2):
            self.one.append(copy(own.at[self.other[i]], first_in.at[i], i, partner[i]))
            self.near.append(copy(totals.at[i], near_in.at[i], 2 + i, near[i]))
            self.far.append(copy(totals.at[i], far_in.at[i], 4 + i, far))
            self.three.append(copy(back.at[i], result.at[self.mine[i]], 6 + i, partner[i]))

    def start(self):
        for i in range(2):
            self.one[i].start()

    def sides(self, i):
        mine, theirs, lead = self.own[self.mine[i]], self.first_in[i], self.lead[i]
        return jnp.where(lead, mine, theirs), jnp.where(lead, theirs, mine)

    def scale(self, state, keeps):
        return jnp.concatenate(
            [state[j * BLOCK : (j + 1) * BLOCK] * keeps[2 * BLOCK + j : 2 * BLOCK + j + 1] for j in range(2)]
        )

    def pair_totals(self):
        for i in range(2):
            self.one[i].wait_recv()
            lead, trail = self.sides(i)
            self.totals[i, : 2 * BLOCK] = lead[: 2 * BLOCK] + self.scale(trail, lead)
            self.totals[i, 2 * BLOCK :] = lead[2 * BLOCK :] * trail[2 * BLOCK :]
            self.near[i].start()
            self.far[i].start()

    def edges(self):
        for i in range(2):
            self.near[i].wait_recv()
            self.far[i].wait_recv()
            near = self.near_in[i]
            entering = near[: 2 * BLOCK] + self.scale(self.far_in[i], near)
            _, trail = self.sides(i)
            at_lead = trail[: 2 * BLOCK] + self.scale(entering, trail)
            self.result[self.mine[i]] = jnp.where(self.lead[i], at_lead, entering)
            self.back[i] = jnp.where(self.lead[i], entering, at_lead)
            self.three[i].start()

    def finish(self):
        for i in range(2):
            self.three[i].wait_recv()
        for i in range(2):
            for copies in (self.one, self.near, self.far, self.three):
                copies[i].wait_send()


def state_rows(head):
    return head // 2, slice(head % 2 * BLOCK, (head % 2 + 1) * BLOCK)


def main_kernel(
    full_width,
    lengths, rates, gain, queries, keys, values, out_grad,
    normed, grad_query, key_part, value_part, key_out, value_out, carried_local, beyond, after,
    query, key, value, cotangent, raw, weights, probs, query_in, grad_raw, state_local, state_half,
    running, entering_gain, leaving_gain, keeping, before, documents,
    own_f, first_f, totals_f, near_f, far_f, back_f, entering,
    own_b, first_b, totals_b, near_b, far_b, back_b,
    sums, sums_in, sums_all,
    load_sem, send_f, recv_f, send_b, recv_b, send_h, recv_h,
):
    heads, blocks = 8, 8
    x, z, head = lax.axis_index("x"), lax.axis_index("z"), lax.axis_index("head")
    me = x * 4 + z
    loads = [
        pltpu.make_async_copy(source, target, load_sem.at[i])
        for i, (source, target) in enumerate(
            ((keys, key), (values, value), (queries, query), (out_grad, cotangent))
        )
    ]
    for load in loads:
        load.start()
    barrier = pltpu.get_barrier_semaphore()
    peers = [place(me + step, head) for step in (1, -1, 3, -3, 4, -4)]
    peers += [(x, z, lax.rem(head + j, 8)) for j in range(1, 8)]
    for peer in peers:
        pl.semaphore_signal(barrier, inc=1, device_id=peer, device_id_type=MESH)

    lane = lax.broadcasted_iota(jnp.int32, (BLOCK, BLOCK), 1)
    sublane = lax.broadcasted_iota(jnp.int32, (BLOCK, BLOCK), 0)
    upto = (sublane <= lane).astype(F32).astype(BF16)
    rate = jnp.concatenate([rates[:, lanes_of(b)] for b in range(blocks)])
    top = rate.astype(BF16)
    rest = rate - top.astype(F32)
    middle = rest.astype(BF16)
    low = (rest - middle.astype(F32)).astype(BF16)
    pieces = dot(jnp.concatenate([top, middle, low]), upto)
    count = heads * blocks
    run = pieces[:count] + pieces[count : 2 * count] + pieces[2 * count :]
    block_start = (x * 4 + z) * (blocks * BLOCK) + BLOCK * lax.broadcasted_iota(jnp.int32, (blocks, BLOCK), 0)
    places = block_start + lax.broadcasted_iota(jnp.int32, (blocks, BLOCK), 1)
    doc = jnp.zeros((blocks, BLOCK), jnp.int32)
    doc_first, doc_last = doc, doc
    end = jnp.int32(0)
    for i in range(lengths.shape[0]):
        end = end + lengths[i]
        doc += (places >= end).astype(jnp.int32)
        doc_first += (block_start - 1 >= end).astype(jnp.int32)
        doc_last += (block_start + (BLOCK - 1) >= end).astype(jnp.int32)
    doc_first = jnp.where(block_start > 0, doc_first, -1)
    documents[...] = doc.astype(F32)
    enter_mask = (doc == doc_first).astype(F32)
    leave_mask = (doc == doc_last).astype(F32)
    keep_mask = (doc_last == doc_first).astype(F32)
    so_far = jnp.ones((heads, BLOCK), F32)
    for b in range(blocks):
        run_b = run[b * heads : (b + 1) * heads]
        total = jnp.broadcast_to(run_b[:, BLOCK - 1 :], (heads, BLOCK))
        running[b] = run_b
        entering_gain[b] = jnp.exp(run_b) * enter_mask[b : b + 1]
        leaving_gain[b] = jnp.exp(total - run_b) * leave_mask[b : b + 1]
        keep = jnp.exp(total) * keep_mask[b : b + 1]
        keeping[b] = keep
        before[b] = so_far
        so_far = so_far * keep
    remaining = jnp.ones((heads, BLOCK), F32)
    for b in reversed(range(blocks)):
        after[b] = remaining
        remaining = remaining * keeping[b]
    for s in range(4):
        tile = jnp.concatenate([so_far[2 * s : 2 * s + 2], jnp.zeros((6, BLOCK), F32)])
        own_f[s, 2 * BLOCK :] = tile
        own_b[s, 2 * BLOCK :] = tile

    forward = Exchange(1, own_f, first_f, totals_f, near_f, far_f, back_f, entering, send_f, recv_f)
    backward = Exchange(-1, own_b, first_b, totals_b, near_b, far_b, back_b, beyond, send_b, recv_b)

    loads[0].wait()
    loads[1].wait()
    for h in range(heads):
        state = jnp.zeros((BLOCK, BLOCK), F32)
        for b in range(blocks):
            low_row = b * BLOCK
            key_t = jnp.transpose(key[low_row : low_row + BLOCK, lanes_of(h)]).astype(F32)
            key_t = (key_t * leaving_gain[b, h : h + 1]).astype(BF16)
            state_local[b, h] = state
            state = keeping[b, h : h + 1] * state + dot(key_t, value[low_row : low_row + BLOCK, lanes_of(h)])
        s, part = state_rows(h)
        own_f[s, part] = state
    pl.semaphore_wait(barrier, len(peers))
    forward.start()
    loads[2].wait()
    loads[3].wait()

    def scores(b, carry):
        rows = rows_of(b)
        doc_row = documents[pl.ds(b, 1), :]
        same = (sublane >= lane) & (as_columns(doc_row) == jnp.broadcast_to(doc_row, (BLOCK, BLOCK)))
        bias = jnp.where(same, 0.0, MASKED)
        for h in range(heads):
            lanes = lanes_of(h)
            query_b, key_b = query[rows, lanes], key[rows, lanes]
            run_row = running[b, h : h + 1]
            weight = jnp.exp(as_columns(run_row) - run_row + bias)
            weights[b, h] = weight
            probs[rows, lanes] = (dot(query_b, key_b, 1, 1) * weight).astype(BF16)
            enter = as_columns(entering_gain[b, h : h + 1])
            query_in[rows, lanes] = (query_b.astype(F32) * enter).astype(BF16)
            leave = as_columns(leaving_gain[b, h : h + 1])
            key_out[rows, lanes] = (key_b.astype(F32) * leave).astype(BF16)
            value_out[rows, lanes] = (value[rows, lanes].astype(F32) * leave).astype(BF16)
        return carry

    lax.fori_loop(0, 4, scores, 0)
    forward.pair_totals()
    lax.fori_loop(4, 8, scores, 0)
    forward.edges()
    forward.finish()

    def finish_raw(b, carry):
        rows = rows_of(b)
        squares = jnp.zeros((BLOCK, BLOCK), F32)
        projected = jnp.zeros((BLOCK, BLOCK), F32)
        for h in range(heads):
            lanes = lanes_of(h)
            s, part = state_rows(h)
            state = (state_local[b, h] + before[b, h : h + 1] * entering[s, part]).astype(BF16)
            state_half[b, h] = state
            left = jnp.concatenate([probs[rows, lanes], query_in[rows, lanes]], axis=1)
            right = jnp.concatenate([value[rows, lanes], state])
            out = dot(left, right)
            raw[rows, lanes] = out
            squares += out * out
            projected += out * (cotangent[rows, lanes].astype(F32) * gain[:, lanes])
        sums[0, pl.ds(b, 1)] = jnp.sum(jnp.transpose(squares), axis=0, keepdims=True)
        sums[1, pl.ds(b, 1)] = jnp.sum(jnp.transpose(projected), axis=0, keepdims=True)
        return carry

    lax.fori_loop(0, blocks, finish_raw, 0)
    shares = []
    for j in range(1, 8):
        shares.append(
            pltpu.make_async_remote_copy(
                src_ref=sums,
                dst_ref=sums_in.at[j - 1],
                send_sem=send_h.at[j - 1],
                recv_sem=recv_h.at[j - 1],
                device_id=(x, z, lax.rem(head + j, 8)),
                device_id_type=MESH,
            )
        )
        shares[-1].start()
    total = sums[...]
    for j in range(7):
        shares[j].wait_recv()
        total = total + sums_in[j]
    inverse = lax.rsqrt(total[0] / full_width + epsilon)
    sums_all[0] = inverse
    sums_all[1] = inverse * inverse * inverse * total[1] / full_width
    for j in range(7):
        shares[j].wait_send()

    for h in range(heads):
        s, part = state_rows(h)
        own_b[s, part] = jnp.zeros((BLOCK, BLOCK), F32)

    def norm(step, carry):
        b = blocks - 1 - step
        rows = rows_of(b)
        inverse = as_columns(sums_all[0, pl.ds(b, 1)])
        pull = as_columns(sums_all[1, pl.ds(b, 1)])
        for h in range(heads):
            lanes = lanes_of(h)
            out, gain_h = raw[rows, lanes], gain[:, lanes]
            normed[rows, lanes] = (out * inverse * gain_h).astype(BF16)
            scaled = cotangent[rows, lanes].astype(F32) * gain_h
            grad = (inverse * scaled - out * pull).astype(BF16)
            grad_raw[rows, lanes] = grad
            s, part = state_rows(h)
            carried = own_b[s, part]
            carried_local[b, h] = carried
            own_b[s, part] = keeping[b, h : h + 1] * carried + dot(jnp.transpose(query_in[rows, lanes]), grad)
        return carry

    lax.fori_loop(0, blocks, norm, 0)
    backward.start()

    def gradients(b, carry):
        rows = rows_of(b)
        for h in range(heads):
            lanes = lanes_of(h)
            grad = grad_raw[rows, lanes]
            mixed = (dot(grad, value[rows, lanes], 1, 1) * weights[b, h]).astype(BF16)
            enter = as_columns(entering_gain[b, h : h + 1])
            across = dot(grad, state_half[b, h], 1, 1)
            grad_query[rows, lanes] = (dot(mixed, key[rows, lanes]) + enter * across).astype(BF16)
            key_part[rows, lanes] = dot(jnp.transpose(mixed), query[rows, lanes])
            value_part[rows, lanes] = dot(jnp.transpose(probs[rows, lanes]), grad)
        return carry

    lax.fori_loop(0, 3, gradients, 0)
    backward.pair_totals()
    lax.fori_loop(3, 6, gradients, 0)
    backward.edges()
    lax.fori_loop(6, 8, gradients, 0)
    backward.finish()


def last_kernel(
    normed_in, query_in, key_part, value_part, key_out, value_out, carried_local, beyond, after,
    normed, grad_query, grad_key, grad_value,
    key_rows, value_rows, pass_sem, key_sem, value_sem,
):
    heads, blocks = 8, 8
    passes = [
        pltpu.make_async_copy(normed_in, normed, pass_sem.at[0]),
        pltpu.make_async_copy(query_in, grad_query, pass_sem.at[1]),
    ]
    for copy in passes:
        copy.start()

    def stores(b):
        rows = rows_of(b)
        return (
            pltpu.make_async_copy(key_rows.at[rows], grad_key.at[rows], key_sem.at[b]),
            pltpu.make_async_copy(value_rows.at[rows], grad_value.at[rows], value_sem.at[b]),
        )

    def block(b, carry):
        rows = rows_of(b)
        for h in range(heads):
            lanes = lanes_of(h)
            s, part = state_rows(h)
            carried = (carried_local[b, h] + after[b, h : h + 1] * beyond[s, part]).astype(BF16)
            key_rows[rows, lanes] = (key_part[rows, lanes] + dot(value_out[rows, lanes], carried, 1, 1)).astype(BF16)
            value_rows[rows, lanes] = (value_part[rows, lanes] + dot(key_out[rows, lanes], carried)).astype(BF16)
        for copy in stores(b):
            copy.start()
        return carry

    lax.fori_loop(0, blocks, block, 0)
    for copy in passes:
        copy.wait()

    def settle(b, carry):
        for copy in stores(b):
            copy.wait()
        return carry

    lax.fori_loop(0, blocks, settle, 0)


def body(queries, keys, values, log_decay, gain, lengths, out_grad):
    rows, width = queries.shape
    full_width = width * lax.axis_size("head")
    vmem = pl.BlockSpec(memory_space=pltpu.VMEM)
    hbm = pl.BlockSpec(memory_space=pl.ANY)
    wide = (rows, width)
    tiles = (8, 8, BLOCK, BLOCK)
    small = (8, 8, BLOCK)
    slab = pltpu.VMEM((2, SLAB, BLOCK), F32)
    own = pltpu.VMEM((4, SLAB, BLOCK), F32)
    pair = pltpu.VMEM((2, 2 * BLOCK, BLOCK), F32)
    edge = pltpu.VMEM((4, 2 * BLOCK, BLOCK), F32)
    wires = [own, slab, slab, slab, slab, pair]
    handed = (
        pltpu.VMEM(wide, BF16),
        pltpu.VMEM(wide, BF16),
        pltpu.VMEM(wide, F32),
        pltpu.VMEM(wide, F32),
        pltpu.VMEM(wide, BF16),
        pltpu.VMEM(wide, BF16),
        pltpu.VMEM(tiles, F32),
        edge,
        pltpu.VMEM(small, F32),
    )
    dma = pltpu.SemaphoreType.DMA
    found = pl.pallas_call(
        functools.partial(main_kernel, full_width),
        out_shape=handed,
        in_specs=[pl.BlockSpec(memory_space=pltpu.SMEM), vmem, vmem, hbm, hbm, hbm, hbm],
        out_specs=(vmem,) * len(handed),
        scratch_shapes=[
            pltpu.VMEM(wide, BF16),
            pltpu.VMEM(wide, BF16),
            pltpu.VMEM(wide, BF16),
            pltpu.VMEM(wide, BF16),
            pltpu.VMEM(wide, F32),
            pltpu.VMEM(tiles, F32),
            pltpu.VMEM(wide, BF16),
            pltpu.VMEM(wide, BF16),
            pltpu.VMEM(wide, BF16),
            pltpu.VMEM(tiles, F32),
            pltpu.VMEM(tiles, BF16),
            pltpu.VMEM(small, F32),
            pltpu.VMEM(small, F32),
            pltpu.VMEM(small, F32),
            pltpu.VMEM(small, F32),
            pltpu.VMEM(small, F32),
            pltpu.VMEM((8, BLOCK), F32),
            *wires,
            edge,
            *wires,
            pltpu.VMEM((2, 8, BLOCK), F32),
            pltpu.VMEM((7, 2, 8, BLOCK), F32),
            pltpu.VMEM((2, 8, BLOCK), F32),
            dma((4,)),
            dma((8,)),
            dma((8,)),
            dma((8,)),
            dma((8,)),
            dma((7,)),
            dma((7,)),
        ],
        compiler_params=pltpu.CompilerParams(
            collective_id=0, has_side_effects=True, vmem_limit_bytes=38 * 2**20
        ),
        name="main_kernel",
    )(lengths, log_decay.T, gain.reshape(1, width), queries, keys, values, out_grad)
    return pl.pallas_call(
        last_kernel,
        out_shape=(jax.ShapeDtypeStruct(wide, BF16),) * 4,
        in_specs=[vmem] * len(handed),
        out_specs=(hbm,) * 4,
        scratch_shapes=[
            pltpu.VMEM(wide, BF16),
            pltpu.VMEM(wide, BF16),
            dma((2,)),
            dma((8,)),
            dma((8,)),
        ],
        compiler_params=pltpu.CompilerParams(vmem_limit_bytes=8 * 2**20),
        name="last_kernel",
    )(*found)


def solution(mesh):
    split = Mesh(mesh.devices.reshape(4, 4, mesh.shape["head"]), ("x", "z", "head"))
    wide = P(SEQ, "head")
    return jax.shard_map(
        body,
        mesh=split,
        in_specs=(wide, wide, wide, wide, P("head"), P(), wide),
        out_specs=(wide,) * 4,
        check_vma=False,
    )
```

profile of v0, /device:TPU:0, one launch (start us, length us, event | category | flops | bytes accessed | tf_op | source)
XLA Modules:
  0.0 69.7 jit_solution(3504110147059228635)
XLA Ops:
  0.6 65.1 %main_kernel.1 = (bf16[1024,1024]{1,0:T(8,128)(2,1)S(1)}, bf16[1024,1024]{1,0:T(8,128)(2,1)S(1)}, f32[1024,1024]{1,0:T(8,128)S(1)}, f32[1024,1024]{1,0:T(8,128)S...) custom-call(s32[8]{0:T(128)} %lengths.1, ...), custom_call_target="tpu_custom_call" | custom-call | tf_op jit(solution)/shard_map/main_kernel/pallas_call | solution.py:400
  65.8 3.9 %last_kernel.1 = (bf16[1024,1024]{1,0:T(8,128)(2,1)}, bf16[1024,1024]{1,0:T(8,128)(2,1)}, bf16[1024,1024]{1,0:T(8,128)(2,1)}, bf16[1024,1024]{1,0:T(8,128)(2,1)}) custom-call(bf16[1024,1024]{1,0:T(8,128)(2,1)S(1)} %get-tuple-element.13.normed_in, bf16[1024,1024]{1,0:T(8,128)(2,1)S(1)} %get-tuple-element.14.query_in, ...), custom_call_target="tpu_custom_call" | custom-call | tf_op jit(solution)/shard_map/last_kernel/pallas_call | solution.py:442
where the time goes:
time: 69.9 us; the launch traced here: 69.7 us
  Pallas kernels  69 us (99%)
    pallas_call x1, Pallas kernels, body(): pl.pallas_call(functools.partial(main_kernel, full_width), out_shape=hand...  65.1 us
    pallas_call x1, Pallas kernels, body(): pl.pallas_call(last_kernel, out_shape=(jax.ShapeDtypeStruct(wide, BF16),)...  3.91 us

commit v1 on v0

v1 whole, which is shorter than its diff:
```python
import functools

import jax
import jax.numpy as jnp
from jax import lax
from jax.experimental import pallas as pl
from jax.experimental.pallas import tpu as pltpu
from jax.sharding import Mesh
from jax.sharding import PartitionSpec as P

BLOCK = 128
HEADS = 8
BLOCKS = 8
SEQ = ("x", "z")
MESH = pl.DeviceIdType.MESH
F32 = jnp.float32
BF16 = jnp.bfloat16
epsilon = 1e-06
MASKED = -1e30
SLAB = BLOCK + 8


def dot(left, right, left_axis=1, right_axis=0):
    dims = (((left_axis,), (right_axis,)), ((), ()))
    return lax.dot_general(left, right, dims, preferred_element_type=F32)


def rows_of(block):
    return pl.ds(pl.multiple_of(block * BLOCK, BLOCK), BLOCK)


def static_rows(block):
    return slice(block * BLOCK, (block + 1) * BLOCK)


def as_columns(row):
    return jnp.transpose(jnp.broadcast_to(row, (BLOCK, BLOCK)))


def place(linear, head):
    linear = lax.rem(linear + 32, 16)
    return (lax.div(linear, 4), lax.rem(linear, 4), head)


class Exchange:
    def __init__(self, step, own, first_in, totals, near_in, far_in, back, result, send, recv):
        self.own, self.first_in, self.totals, self.near_in = own, first_in, totals, near_in
        self.far_in, self.back, self.result = far_in, back, result
        x, z, head = lax.axis_index("x"), lax.axis_index("z"), lax.axis_index("head")
        me = x * 4 + z
        odd = lax.rem(z, 2)
        half = jnp.where((z == 0) | (z == 3), 0, 1)
        self.mine = [4 * half + k for k in range(4)]
        self.other = [4 * (1 - half) + k for k in range(4)]
        self.lead = odd == (1 if step == 1 else 0)
        partner = me + 1 - 2 * odd
        near_to = me + step * jnp.where(self.lead, 1, 3)
        near_from = me - step * jnp.where(self.lead, 3, 1)
        far_to, far_from = me + 4 * step, me - 4 * step

        def exists(linear):
            return (linear >= 0) & (linear < 16)

        self.near_out, self.far_out = exists(near_to), exists(far_to)
        self.near_comes, self.far_comes = exists(near_from), exists(far_from)

        def copy(source, target, index, linear):
            return pltpu.make_async_remote_copy(
                src_ref=source,
                dst_ref=target,
                send_sem=send.at[index],
                recv_sem=recv.at[index],
                device_id=place(linear, head),
                device_id_type=MESH,
            )

        self.one, self.near, self.far, self.three = [], [], [], []
        for k in range(4):
            self.one.append(copy(own.at[self.other[k]], first_in.at[k], k, partner))
            self.near.append(copy(totals.at[k], near_in.at[k], 4 + k, near_to))
            self.far.append(copy(totals.at[k], far_in.at[k], 8 + k, far_to))
            self.three.append(copy(back.at[k], result.at[self.mine[k]], 12 + k, partner))

    def prepare(self):
        @pl.when(jnp.logical_not(self.near_comes))
        def _():
            self.near_in[...] = jnp.zeros_like(self.near_in)

        @pl.when(jnp.logical_not(self.far_comes))
        def _():
            self.far_in[...] = jnp.zeros_like(self.far_in)

    def start(self, k):
        self.one[k].start()

    def sides(self, k):
        mine, theirs = self.own[self.mine[k]], self.first_in[k]
        return jnp.where(self.lead, mine, theirs), jnp.where(self.lead, theirs, mine)

    def pair_totals(self, k):
        self.one[k].wait_recv()
        lead, trail = self.sides(k)
        self.totals[k, :BLOCK] = lead[:BLOCK] + trail[:BLOCK] * lead[BLOCK : BLOCK + 1]
        self.totals[k, BLOCK:] = lead[BLOCK:] * trail[BLOCK:]
        pl.when(self.near_out)(self.near[k].start)
        pl.when(self.far_out)(self.far[k].start)

    def edges(self, k):
        pl.when(self.near_comes)(self.near[k].wait_recv)
        pl.when(self.far_comes)(self.far[k].wait_recv)
        near, far = self.near_in[k], self.far_in[k]
        entering = near[:BLOCK] + far[:BLOCK] * near[BLOCK : BLOCK + 1]
        _, trail = self.sides(k)
        at_lead = trail[:BLOCK] + entering * trail[BLOCK : BLOCK + 1]
        self.back[k] = jnp.where(self.lead, entering, at_lead)
        self.three[k].start()
        self.result[self.mine[k]] = jnp.where(self.lead, at_lead, entering)

    def arrive(self, k):
        self.three[k].wait_recv()

    def finish(self):
        for k in range(4):
            self.one[k].wait_send()
            pl.when(self.near_out)(self.near[k].wait_send)
            pl.when(self.far_out)(self.far[k].wait_send)
            self.three[k].wait_send()


def main_kernel(
    full_width,
    lengths, rates, gain, queries, keys, values, out_grad,
    normed, grad_query, key_part, value_part, key_dev, value_dev, beyond,
    query, key, value, cotangent, raw, scaled, weights, probs_t, query_in_t, query_dev, query_dev_t,
    key_in, grad_raw, state_local, state_half_t, chain, inverse_at, pull_at,
    running, entering_gain, leaving_gain, keeping, before, after, documents,
    own_f, first_f, totals_f, near_f, far_f, back_f, entering,
    own_b, first_b, totals_b, near_b, far_b, back_b,
    sums, sums_in,
    load_sem, send_f, recv_f, send_b, recv_b, send_h, recv_h,
):
    value_in = cotangent
    x, z, head = lax.axis_index("x"), lax.axis_index("z"), lax.axis_index("head")
    me = x * 4 + z
    loads = [
        pltpu.make_async_copy(source, target, load_sem.at[i])
        for i, (source, target) in enumerate(
            ((keys, key), (values, value), (queries, query), (out_grad, cotangent))
        )
    ]
    loads[0].start()
    loads[1].start()
    barrier = pltpu.get_barrier_semaphore()
    peers = [place(me + step, head) for step in (1, -1, 3, -3, 4, -4)]
    peers += [(x, z, lax.rem(head + j, 8)) for j in range(1, 8)]
    for peer in peers:
        pl.semaphore_signal(barrier, inc=1, device_id=peer, device_id_type=MESH)

    lane = lax.broadcasted_iota(jnp.int32, (BLOCK, BLOCK), 1)
    sublane = lax.broadcasted_iota(jnp.int32, (BLOCK, BLOCK), 0)
    upto = (sublane <= lane).astype(F32).astype(BF16)
    rate = jnp.concatenate([rates[:, static_rows(b)] for b in range(BLOCKS)])
    top = rate.astype(BF16)
    rest = rate - top.astype(F32)
    middle = rest.astype(BF16)
    low = (rest - middle.astype(F32)).astype(BF16)
    pieces = dot(jnp.concatenate([top, middle, low]), upto)
    count = HEADS * BLOCKS
    run = pieces[:count] + pieces[count : 2 * count] + pieces[2 * count :]
    block_start = me * (BLOCKS * BLOCK) + BLOCK * lax.broadcasted_iota(jnp.int32, (BLOCKS, BLOCK), 0)
    places = block_start + lax.broadcasted_iota(jnp.int32, (BLOCKS, BLOCK), 1)
    doc = jnp.zeros((BLOCKS, BLOCK), jnp.int32)
    doc_first, doc_last = doc, doc
    end = jnp.int32(0)
    for i in range(lengths.shape[0]):
        end = end + lengths[i]
        doc += (places >= end).astype(jnp.int32)
        doc_first += (block_start - 1 >= end).astype(jnp.int32)
        doc_last += (block_start + (BLOCK - 1) >= end).astype(jnp.int32)
    doc_first = jnp.where(block_start > 0, doc_first, -1)
    documents[...] = doc.astype(F32)
    enter_mask = (doc == doc_first).astype(F32)
    leave_mask = (doc == doc_last).astype(F32)
    keep_mask = (doc_last == doc_first).astype(F32)
    so_far = jnp.ones((HEADS, BLOCK), F32)
    for b in range(BLOCKS):
        run_b = run[b * HEADS : (b + 1) * HEADS]
        total = jnp.broadcast_to(run_b[:, BLOCK - 1 :], (HEADS, BLOCK))
        running[b] = run_b
        entering_gain[b] = jnp.exp(run_b) * enter_mask[b : b + 1]
        leaving_gain[b] = jnp.exp(total - run_b) * leave_mask[b : b + 1]
        keep = jnp.exp(total) * keep_mask[b : b + 1]
        keeping[b] = keep
        before[b] = so_far
        so_far = so_far * keep
    remaining = jnp.ones((HEADS, BLOCK), F32)
    for b in reversed(range(BLOCKS)):
        after[b] = remaining
        remaining = remaining * keeping[b]
    for h in range(HEADS):
        tile = jnp.broadcast_to(so_far[h : h + 1], (8, BLOCK))
        own_f[h, BLOCK:] = tile
        own_b[h, BLOCK:] = tile

    forward = Exchange(1, own_f, first_f, totals_f, near_f, far_f, back_f, entering, send_f, recv_f)
    backward = Exchange(-1, own_b, first_b, totals_b, near_b, far_b, back_b, beyond, send_b, recv_b)

    forward.prepare()
    backward.prepare()

    loads[0].wait()
    loads[1].wait()
    loads[2].start()
    loads[3].start()
    for turn, h in enumerate(forward.other + forward.mine):
        lanes = rows_of(h)
        pieces = []
        for b in range(BLOCKS):
            leave = leaving_gain[b, pl.ds(h, 1)] * after[b, pl.ds(h, 1)]
            pieces.append((jnp.transpose(key[static_rows(b), lanes]).astype(F32) * leave).astype(BF16))
        own_f[h, :BLOCK] = dot(jnp.concatenate(pieces, axis=1), value[:, lanes])
        if turn == 0:
            pl.semaphore_wait(barrier, len(peers))
        if turn < 4:
            forward.start(turn)
    chain[...] = jnp.zeros_like(chain)
    loads[2].wait()
    loads[3].wait()

    def local(b, carry):
        rows = rows_of(b)
        doc_row = documents[pl.ds(b, 1), :]
        same = (sublane >= lane) & (as_columns(doc_row) == jnp.broadcast_to(doc_row, (BLOCK, BLOCK)))
        bias = jnp.where(same, 0.0, MASKED)
        for h in range(HEADS):
            lanes = static_rows(h)
            query_b, key_b, value_b = query[rows, lanes], key[rows, lanes], value[rows, lanes]
            run_row = running[b, h : h + 1]
            weight = jnp.exp(as_columns(run_row) - run_row + bias)
            weights[b, h] = weight
            probs = (dot(query_b, key_b, 1, 1) * weight).astype(BF16)
            probs_t[b, h] = jnp.transpose(probs)
            query_e = query_b.astype(F32) * as_columns(entering_gain[b, h : h + 1])
            query_in = query_e.astype(BF16)
            query_in_t[b, h] = jnp.transpose(query_in)
            query_d = (query_e * before[b, h : h + 1]).astype(BF16)
            query_dev[rows, lanes] = query_d
            query_dev_t[h, :, rows] = jnp.transpose(query_d)
            leave = as_columns(leaving_gain[b, h : h + 1])
            after_row = after[b, h : h + 1]
            key_l = key_b.astype(F32) * leave
            key_lb = key_l.astype(BF16)
            key_in[rows, lanes] = key_lb
            key_dev[rows, lanes] = (key_l * after_row).astype(BF16)
            scaled[rows, lanes] = cotangent[rows, lanes].astype(F32) * gain[:, lanes]
            value_l = value_b.astype(F32) * leave
            value_in[rows, lanes] = value_l.astype(BF16)
            value_dev[rows, lanes] = (value_l * after_row).astype(BF16)
            state = chain[h]
            state_local[b, h] = state
            raw[rows, lanes] = dot(
                jnp.concatenate([probs, query_in], axis=1), jnp.concatenate([value_b, state.astype(BF16)])
            )
            chain[h] = keeping[b, h : h + 1] * state + dot(jnp.transpose(key_lb), value_b)
        return carry

    lax.fori_loop(0, 3, local, 0)
    forward.pair_totals(0)
    forward.pair_totals(1)
    lax.fori_loop(3, 5, local, 0)
    forward.pair_totals(2)
    forward.pair_totals(3)
    lax.fori_loop(5, 8, local, 0)
    squares, projected = inverse_at, pull_at
    squares[...] = jnp.zeros_like(squares)
    projected[...] = jnp.zeros_like(projected)

    def finish_raw(h):
        lanes = rows_of(h)
        added = dot(query_dev[:, lanes], entering[h].astype(BF16))
        for b in range(BLOCKS):
            rows = static_rows(b)
            out = raw[rows, lanes] + added[rows]
            raw[rows, lanes] = out
            squares[b] += out * out
            projected[b] += out * scaled[rows, lanes]

    for k in range(4):
        forward.edges(k)
        finish_raw(forward.mine[k])
    for k in range(4):
        forward.arrive(k)
        finish_raw(forward.other[k])
    for b in range(BLOCKS):
        sums[0, b : b + 1] = jnp.sum(jnp.transpose(squares[b]), axis=0, keepdims=True)
        sums[1, b : b + 1] = jnp.sum(jnp.transpose(projected[b]), axis=0, keepdims=True)
    shares = []
    for j in range(1, 8):
        shares.append(
            pltpu.make_async_remote_copy(
                src_ref=sums,
                dst_ref=sums_in.at[j - 1],
                send_sem=send_h.at[j - 1],
                recv_sem=recv_h.at[j - 1],
                device_id=(x, z, lax.rem(head + j, 8)),
                device_id_type=MESH,
            )
        )
        shares[-1].start()
    forward.finish()
    chain[...] = jnp.zeros_like(chain)

    def whole_states(b, carry):
        for h in range(HEADS):
            state = state_local[b, h] + before[b, h : h + 1] * entering[h]
            state_half_t[b, h] = jnp.transpose(state.astype(BF16))
        return carry

    lax.fori_loop(0, BLOCKS, whole_states, 0)
    total = sums[...]
    for j in range(7):
        shares[j].wait_recv()
        total = total + sums_in[j]
    inverse = lax.rsqrt(total[0] / full_width + epsilon)
    pull = inverse * inverse * inverse * total[1] / full_width
    for b in range(BLOCKS):
        inverse_at[b] = as_columns(inverse[b : b + 1])
        pull_at[b] = as_columns(pull[b : b + 1])
    for turn, h in enumerate(backward.other + backward.mine):
        lanes = rows_of(h)
        pieces = []
        for b in range(BLOCKS):
            rows = static_rows(b)
            grad = (inverse_at[b] * scaled[rows, lanes] - raw[rows, lanes] * pull_at[b]).astype(BF16)
            grad_raw[rows, lanes] = grad
            pieces.append(grad)
        own_b[h, :BLOCK] = dot(query_dev_t[h], jnp.concatenate(pieces))
        if turn < 4:
            backward.start(turn)
    for j in range(7):
        shares[j].wait_send()

    def gradients(step, carry):
        b = BLOCKS - 1 - step
        rows = rows_of(b)
        for h in range(HEADS):
            lanes = static_rows(h)
            grad = grad_raw[rows, lanes]
            mixed = (dot(grad, value[rows, lanes], 1, 1) * weights[b, h]).astype(BF16)
            grad_in = (grad.astype(F32) * as_columns(entering_gain[b, h : h + 1])).astype(BF16)
            grad_query[rows, lanes] = dot(
                jnp.concatenate([mixed, grad_in], axis=1),
                jnp.concatenate([key[rows, lanes], state_half_t[b, h]]),
            ).astype(BF16)
            carried = chain[h]
            carried_half = carried.astype(BF16)
            key_part[rows, lanes] = dot(
                jnp.concatenate([jnp.transpose(mixed), value_in[rows, lanes]], axis=1),
                jnp.concatenate([query[rows, lanes], jnp.transpose(carried_half)]),
            )
            value_part[rows, lanes] = dot(
                jnp.concatenate([probs_t[b, h], key_in[rows, lanes]], axis=1),
                jnp.concatenate([grad, carried_half]),
            )
            chain[h] = keeping[b, h : h + 1] * carried + dot(query_in_t[b, h], grad)
            normed[rows, lanes] = (raw[rows, lanes] * inverse_at[b] * gain[:, lanes]).astype(BF16)
        return carry

    lax.fori_loop(0, 2, gradients, 0)
    backward.pair_totals(0)
    backward.pair_totals(1)
    lax.fori_loop(2, 3, gradients, 0)
    backward.pair_totals(2)
    backward.pair_totals(3)
    lax.fori_loop(3, 6, gradients, 0)
    backward.edges(0)
    lax.fori_loop(6, 7, gradients, 0)
    backward.edges(1)
    lax.fori_loop(7, 8, gradients, 0)
    backward.edges(2)
    backward.edges(3)
    for k in range(4):
        backward.arrive(k)
    backward.finish()


def last_kernel(
    normed_in, query_in, key_part, value_part, key_dev, value_dev, beyond,
    normed, grad_query, grad_key, grad_value,
    key_rows, value_rows, pass_sem, key_sem, value_sem,
):
    passes = [
        pltpu.make_async_copy(normed_in, normed, pass_sem.at[0]),
        pltpu.make_async_copy(query_in, grad_query, pass_sem.at[1]),
    ]
    for copy in passes:
        copy.start()

    def stores(b):
        rows = rows_of(b)
        return (
            pltpu.make_async_copy(key_rows.at[rows], grad_key.at[rows], key_sem.at[b]),
            pltpu.make_async_copy(value_rows.at[rows], grad_value.at[rows], value_sem.at[b]),
        )

    def block(b, carry):
        rows = rows_of(b)
        for h in range(HEADS):
            lanes = static_rows(h)
            carried = beyond[h].astype(BF16)
            key_rows[rows, lanes] = (key_part[rows, lanes] + dot(value_dev[rows, lanes], carried, 1, 1)).astype(BF16)
            value_rows[rows, lanes] = (value_part[rows, lanes] + dot(key_dev[rows, lanes], carried)).astype(BF16)
        for copy in stores(b):
            copy.start()
        return carry

    lax.fori_loop(0, BLOCKS, block, 0)
    for copy in passes:
        copy.wait()

    def settle(b, carry):
        for copy in stores(b):
            copy.wait()
        return carry

    lax.fori_loop(0, BLOCKS, settle, 0)


def body(queries, keys, values, log_decay, gain, lengths, out_grad):
    rows, width = queries.shape
    full_width = width * lax.axis_size("head")
    vmem = pl.BlockSpec(memory_space=pltpu.VMEM)
    hbm = pl.BlockSpec(memory_space=pl.ANY)
    wide = (rows, width)
    tiles = (BLOCKS, HEADS, BLOCK, BLOCK)
    small = pltpu.VMEM((BLOCKS, HEADS, BLOCK), F32)
    own = pltpu.VMEM((HEADS, SLAB, BLOCK), F32)
    slab = pltpu.VMEM((4, SLAB, BLOCK), F32)
    states = pltpu.VMEM((HEADS, BLOCK, BLOCK), F32)
    wires = [own, slab, slab, slab, slab, pltpu.VMEM((4, BLOCK, BLOCK), F32)]
    half, full = pltpu.VMEM(wide, BF16), pltpu.VMEM(wide, F32)
    handed = (half, half, full, full, half, half, states)
    dma = pltpu.SemaphoreType.DMA
    found = pl.pallas_call(
        functools.partial(main_kernel, full_width),
        out_shape=handed,
        in_specs=[pl.BlockSpec(memory_space=pltpu.SMEM), vmem, vmem, hbm, hbm, hbm, hbm],
        out_specs=(vmem,) * len(handed),
        scratch_shapes=[
            half, half, half, half, full, full,
            pltpu.VMEM(tiles, F32),
            pltpu.VMEM(tiles, BF16),
            pltpu.VMEM(tiles, BF16),
            half,
            pltpu.VMEM((HEADS, BLOCK, rows), BF16),
            half, half,
            pltpu.VMEM(tiles, F32),
            pltpu.VMEM(tiles, BF16),
            states, states, states,
            small, small, small, small, small, small,
            pltpu.VMEM((BLOCKS, BLOCK), F32),
            *wires,
            states,
            *wires,
            pltpu.VMEM((2, BLOCKS, BLOCK), F32),
            pltpu.VMEM((7, 2, BLOCKS, BLOCK), F32),
            dma((4,)),
            dma((16,)),
            dma((16,)),
            dma((16,)),
            dma((16,)),
            dma((7,)),
            dma((7,)),
        ],
        compiler_params=pltpu.CompilerParams(
            collective_id=0, has_side_effects=True, vmem_limit_bytes=46 * 2**20
        ),
        name="main_kernel",
    )(lengths, log_decay.T, gain.reshape(1, width), queries, keys, values, out_grad)
    return pl.pallas_call(
        last_kernel,
        out_shape=(jax.ShapeDtypeStruct(wide, BF16),) * 4,
        in_specs=[vmem] * len(handed),
        out_specs=(hbm,) * 4,
        scratch_shapes=[half, half, dma((2,)), dma((8,)), dma((8,))],
        compiler_params=pltpu.CompilerParams(vmem_limit_bytes=8 * 2**20),
        name="last_kernel",
    )(*found)


def solution(mesh):
    split = Mesh(mesh.devices.reshape(4, 4, mesh.shape["head"]), ("x", "z", "head"))
    wide = P(SEQ, "head")
    return jax.shard_map(
        body,
        mesh=split,
        in_specs=(wide, wide, wide, wide, P("head"), P(), wide),
        out_specs=(wide,) * 4,
        check_vma=False,
    )
```

time: 69.9 us -> 64.2 us (0.918)
  Pallas kernels: 69 us -> 63.2 us
    pallas_call x1, Pallas kernels: 65.1 us -> 59.4 us  [body(): pl.pallas_call(functools.partial(main_kernel, full_width), out_shape=hand...]
where the time goes in v1:
time: 64.2 us; the launch traced here: 64 us
  Pallas kernels  63.2 us (98%)
  between operations  0.8 us (1%)
    pallas_call x1, Pallas kernels, body(): pl.pallas_call(functools.partial(main_kernel, full_width), out_shape=hand...  59.4 us
    pallas_call x1, Pallas kernels, body(): pl.pallas_call(last_kernel, out_shape=(jax.ShapeDtypeStruct(wide, BF16),)...  3.87 us

profile of v1, /device:TPU:0, one launch (start us, length us, event | category | flops | bytes accessed | tf_op | source)
XLA Modules:
  0.0 64.0 jit_solution(15489166846030219235)
XLA Ops:
  0.6 59.4 %main_kernel.1 = (bf16[1024,1024]{1,0:T(8,128)(2,1)S(1)}, bf16[1024,1024]{1,0:T(8,128)(2,1)S(1)}, f32[1024,1024]{1,0:T(8,128)S(1)}, f32[1024,1024]{1,0:T(8,128)S...) custom-call(s32[8]{0:T(128)} %lengths.1, f32[8,1024]{1,0:T(8,128)} %bitcast.2, ...), custom_call_target="tpu_custom_call" | custom-call | tf_op jit(solution)/shard_map/main_kernel/pallas_call | solution.py:444
  60.0 3.9 %last_kernel.1 = (bf16[1024,1024]{1,0:T(8,128)(2,1)}, bf16[1024,1024]{1,0:T(8,128)(2,1)}, bf16[1024,1024]{1,0:T(8,128)(2,1)}, bf16[1024,1024]{1,0:T(8,128)(2,1)}) custom-call(bf16[1024,1024]{1,0:T(8,128)(2,1)S(1)} %get-tuple-element.11.normed_in, bf16[1024,1024]{1,0:T(8,128)(2,1)S(1)} %get-tuple-element.12.query_in, ...), custom_call_target="tpu_custom_call" | custom-call | tf_op jit(solution)/shard_map/last_kernel/pallas_call | solution.py:480

commit v2 on v1

--- a/solution.py
+++ b/solution.py
@@ -37,58 +37,44 @@
     return jnp.transpose(jnp.broadcast_to(row, (BLOCK, BLOCK)))
 
 
-def place(linear, head):
-    linear = lax.rem(linear + 32, 16)
-    return (lax.div(linear, 4), lax.rem(linear, 4), head)
-
-
 class Exchange:
-    def __init__(self, step, own, first_in, totals, near_in, far_in, back, result, send, recv):
-        self.own, self.first_in, self.totals, self.near_in = own, first_in, totals, near_in
-        self.far_in, self.back, self.result = far_in, back, result
+    def __init__(self, step, own, first_in, totals, mate_in, row, row_in, back, result, send, recv):
+        self.own, self.first_in, self.totals, self.mate_in = own, first_in, totals, mate_in
+        self.row, self.row_in, self.back, self.result = row, row_in, back, result
         x, z, head = lax.axis_index("x"), lax.axis_index("z"), lax.axis_index("head")
-        me = x * 4 + z
         odd = lax.rem(z, 2)
         half = jnp.where((z == 0) | (z == 3), 0, 1)
         self.mine = [4 * half + k for k in range(4)]
         self.other = [4 * (1 - half) + k for k in range(4)]
         self.lead = odd == (1 if step == 1 else 0)
-        partner = me + 1 - 2 * odd
-        near_to = me + step * jnp.where(self.lead, 1, 3)
-        near_from = me - step * jnp.where(self.lead, 3, 1)
-        far_to, far_from = me + 4 * step, me - 4 * step
-
-        def exists(linear):
-            return (linear >= 0) & (linear < 16)
-
-        self.near_out, self.far_out = exists(near_to), exists(far_to)
-        self.near_comes, self.far_comes = exists(near_from), exists(far_from)
-
-        def copy(source, target, index, linear):
+        self.entry = z < 2 if step == 1 else z >= 2
+        self.goes = x < 3 if step == 1 else x > 0
+        self.comes = x > 0 if step == 1 else x < 3
+        partner = (x, z + 1 - 2 * odd, head)
+        mate = (x, 3 - z, head)
+        onward = (lax.rem(x + step + 4, 4), z, head)
+
+        def copy(source, target, index, device):
             return pltpu.make_async_remote_copy(
                 src_ref=source,
                 dst_ref=target,
                 send_sem=send.at[index],
                 recv_sem=recv.at[index],
-                device_id=place(linear, head),
+                device_id=device,
                 device_id_type=MESH,
             )
 
-        self.one, self.near, self.far, self.three = [], [], [], []
+        self.one, self.two, self.on, self.three = [], [], [], []
         for k in range(4):
             self.one.append(copy(own.at[self.other[k]], first_in.at[k], k, partner))
-            self.near.append(copy(totals.at[k], near_in.at[k], 4 + k, near_to))
-            self.far.append(copy(totals.at[k], far_in.at[k], 8 + k, far_to))
+            self.two.append(copy(totals.at[k], mate_in.at[k], 4 + k, mate))
+            self.on.append(copy(row.at[k], row_in.at[k], 8 + k, onward))
             self.three.append(copy(back.at[k], result.at[self.mine[k]], 12 + k, partner))
 
     def prepare(self):
-        @pl.when(jnp.logical_not(self.near_comes))
+        @pl.when(jnp.logical_not(self.comes))
         def _():
-            self.near_in[...] = jnp.zeros_like(self.near_in)
-
-        @pl.when(jnp.logical_not(self.far_comes))
-        def _():
-            self.far_in[...] = jnp.zeros_like(self.far_in)
+            self.row_in[...] = jnp.zeros_like(self.row_in)
 
     def start(self, k):
         self.one[k].start()
@@ -100,16 +86,29 @@
     def pair_totals(self, k):
         self.one[k].wait_recv()
         lead, trail = self.sides(k)
-        self.totals[k, :BLOCK] = lead[:BLOCK] + trail[:BLOCK] * lead[BLOCK : BLOCK + 1]
+        total = lead[:BLOCK] + trail[:BLOCK] * lead[BLOCK : BLOCK + 1]
+        self.totals[k, :BLOCK] = total
         self.totals[k, BLOCK:] = lead[BLOCK:] * trail[BLOCK:]
-        pl.when(self.near_out)(self.near[k].start)
-        pl.when(self.far_out)(self.far[k].start)
+        self.two[k].start()
+
+        @pl.when(jnp.logical_not(self.entry))
+        def _():
+            self.row[k] = total
+            pl.when(self.goes)(self.on[k].start)
+
+    def row_totals(self, k):
+        self.two[k].wait_recv()
+
+        @pl.when(self.entry)
+        def _():
+            mate = self.mate_in[k]
+            self.row[k] = mate[:BLOCK] + self.totals[k, :BLOCK] * mate[BLOCK : BLOCK + 1]
+            pl.when(self.goes)(self.on[k].start)
 
     def edges(self, k):
-        pl.when(self.near_comes)(self.near[k].wait_recv)
-        pl.when(self.far_comes)(self.far[k].wait_recv)
-        near, far = self.near_in[k], self.far_in[k]
-        entering = near[:BLOCK] + far[:BLOCK] * near[BLOCK : BLOCK + 1]
+        pl.when(self.comes)(self.on[k].wait_recv)
+        mate, row = self.mate_in[k], self.row_in[k]
+        entering = jnp.where(self.entry, row, mate[:BLOCK] + row * mate[BLOCK : BLOCK + 1])
         _, trail = self.sides(k)
         at_lead = trail[:BLOCK] + entering * trail[BLOCK : BLOCK + 1]
         self.back[k] = jnp.where(self.lead, entering, at_lead)
@@ -122,9 +121,36 @@
     def finish(self):
         for k in range(4):
             self.one[k].wait_send()
-            pl.when(self.near_out)(self.near[k].wait_send)
-            pl.when(self.far_out)(self.far[k].wait_send)
+            self.two[k].wait_send()
+            pl.when(self.goes)(self.on[k].wait_send)
             self.three[k].wait_send()
+
+    def serve(self, step, plan):
+        for at, name, k in plan:
+            pl.when(step == at)(functools.partial(getattr(self, name), k))
+
+
+FORWARD_PLAN = (
+    (1, "pair_totals", 0),
+    (2, "pair_totals", 1),
+    (3, "pair_totals", 2),
+    (4, "pair_totals", 3),
+    (4, "row_totals", 0),
+    (5, "row_totals", 1),
+    (6, "row_totals", 2),
+)
+BACKWARD_PLAN = (
+    (0, "pair_totals", 0),
+    (1, "pair_totals", 1),
+    (2, "pair_totals", 2),
+    (3, "pair_totals", 3),
+    (3, "row_totals", 0),
+    (4, "row_totals", 1),
+    (4, "row_totals", 2),
+    (5, "row_totals", 3),
+    (5, "edges", 0),
+    (6, "edges", 1),
+)
 
 
 def main_kernel(
@@ -134,8 +160,8 @@
     query, key, value, cotangent, raw, scaled, weights, probs_t, query_in_t, query_dev, query_dev_t,
     key_in, grad_raw, state_local, state_half_t, chain, inverse_at, pull_at,
     running, entering_gain, leaving_gain, keeping, before, after, documents,
-    own_f, first_f, totals_f, near_f, far_f, back_f, entering,
-    own_b, first_b, totals_b, near_b, far_b, back_b,
+    own_f, first_f, totals_f, mate_f, row_f, row_in_f, back_f, entering,
+    own_b, first_b, totals_b, mate_b, row_b, row_in_b, back_b,
     sums, sums_in,
     load_sem, send_f, recv_f, send_b, recv_b, send_h, recv_h,
 ):
@@ -151,7 +177,8 @@
     loads[0].start()
     loads[1].start()
     barrier = pltpu.get_barrier_semaphore()
-    peers = [place(me + step, head) for step in (1, -1, 3, -3, 4, -4)]
+    peers = [(x, z + 1 - 2 * lax.rem(z, 2), head), (x, 3 - z, head)]
+    peers += [(lax.rem(x + step, 4), z, head) for step in (1, 3)]
     peers += [(x, z, lax.rem(head + j, 8)) for j in range(1, 8)]
     for peer in peers:
         pl.semaphore_signal(barrier, inc=1, device_id=peer, device_id_type=MESH)
@@ -202,8 +229,8 @@
         own_f[h, BLOCK:] = tile
         own_b[h, BLOCK:] = tile
 
-    forward = Exchange(1, own_f, first_f, totals_f, near_f, far_f, back_f, entering, send_f, recv_f)
-    backward = Exchange(-1, own_b, first_b, totals_b, near_b, far_b, back_b, beyond, send_b, recv_b)
+    forward = Exchange(1, own_f, first_f, totals_f, mate_f, row_f, row_in_f, back_f, entering, send_f, recv_f)
+    backward = Exchange(-1, own_b, first_b, totals_b, mate_b, row_b, row_in_b, back_b, beyond, send_b, recv_b)
 
     forward.prepare()
     backward.prepare()
@@ -262,15 +289,11 @@
                 jnp.concatenate([probs, query_in], axis=1), jnp.concatenate([value_b, state.astype(BF16)])
             )
             chain[h] = keeping[b, h : h + 1] * state + dot(jnp.transpose(key_lb), value_b)
+        forward.serve(b, FORWARD_PLAN)
         return carry
 
-    lax.fori_loop(0, 3, local, 0)
-    forward.pair_totals(0)
-    forward.pair_totals(1)
-    lax.fori_loop(3, 5, local, 0)
-    forward.pair_totals(2)
-    forward.pair_totals(3)
-    lax.fori_loop(5, 8, local, 0)
+    lax.fori_loop(0, BLOCKS, local, 0)
+    forward.row_totals(3)
     squares, projected = inverse_at, pull_at
     squares[...] = jnp.zeros_like(squares)
     projected[...] = jnp.zeros_like(projected)
@@ -364,19 +387,10 @@
             )
             chain[h] = keeping[b, h : h + 1] * carried + dot(query_in_t[b, h], grad)
             normed[rows, lanes] = (raw[rows, lanes] * inverse_at[b] * gain[:, lanes]).astype(BF16)
+        backward.serve(step, BACKWARD_PLAN)
         return carry
 
-    lax.fori_loop(0, 2, gradients, 0)
-    backward.pair_totals(0)
-    backward.pair_totals(1)
-    lax.fori_loop(2, 3, gradients, 0)
-    backward.pair_totals(2)
-    backward.pair_totals(3)
-    lax.fori_loop(3, 6, gradients, 0)
-    backward.edges(0)
-    lax.fori_loop(6, 7, gradients, 0)
-    backward.edges(1)
-    lax.fori_loop(7, 8, gradients, 0)
+    lax.fori_loop(0, BLOCKS, gradients, 0)
     backward.edges(2)
     backward.edges(3)
     for k in range(4):
@@ -437,7 +451,8 @@
     own = pltpu.VMEM((HEADS, SLAB, BLOCK), F32)
     slab = pltpu.VMEM((4, SLAB, BLOCK), F32)
     states = pltpu.VMEM((HEADS, BLOCK, BLOCK), F32)
-    wires = [own, slab, slab, slab, slab, pltpu.VMEM((4, BLOCK, BLOCK), F32)]
+    part = pltpu.VMEM((4, BLOCK, BLOCK), F32)
+    wires = [own, slab, slab, slab, part, part, part]
     half, full = pltpu.VMEM(wide, BF16), pltpu.VMEM(wide, F32)
     handed = (half, half, full, full, half, half, states)
     dma = pltpu.SemaphoreType.DMA

time: 64.2 us -> 59.9 us (0.933)
  Pallas kernels: 63.2 us -> 59.1 us
    pallas_call x1, Pallas kernels: 59.4 us -> 55.2 us  [body(): pl.pallas_call(functools.partial(main_kernel, full_width), out_shape=hand...]
where the time goes in v2:
time: 59.9 us; the launch traced here: 59.7 us
  Pallas kernels  59.1 us (99%)
  between operations  0.64 us (1%)
    pallas_call x1, Pallas kernels, body(): pl.pallas_call(functools.partial(main_kernel, full_width), out_shape=hand...  55.2 us
    pallas_call x1, Pallas kernels, body(): pl.pallas_call(last_kernel, out_shape=(jax.ShapeDtypeStruct(wide, BF16),)...  3.87 us

profile of v2, /device:TPU:0, one launch (start us, length us, event | category | flops | bytes accessed | tf_op | source)
XLA Modules:
  0.0 59.7 jit_solution(9678383172029438247)
XLA Ops:
  0.6 55.2 %main_kernel.1 = (bf16[1024,1024]{1,0:T(8,128)(2,1)S(1)}, bf16[1024,1024]{1,0:T(8,128)(2,1)S(1)}, f32[1024,1024]{1,0:T(8,128)S(1)}, f32[1024,1024]{1,0:T(8,128)S...) custom-call(s32[8]{0:T(128)} %lengths.1, f32[8,1024]{1,0:T(8,128)} %bitcast.2, ...), custom_call_target="tpu_custom_call" | custom-call | tf_op jit(solution)/shard_map/main_kernel/pallas_call | solution.py:459
  55.9 3.9 %last_kernel.1 = (bf16[1024,1024]{1,0:T(8,128)(2,1)}, bf16[1024,1024]{1,0:T(8,128)(2,1)}, bf16[1024,1024]{1,0:T(8,128)(2,1)}, bf16[1024,1024]{1,0:T(8,128)(2,1)}) custom-call(bf16[1024,1024]{1,0:T(8,128)(2,1)S(1)} %get-tuple-element.11.normed_in, bf16[1024,1024]{1,0:T(8,128)(2,1)S(1)} %get-tuple-element.12.query_in, ...), custom_call_target="tpu_custom_call" | custom-call | tf_op jit(solution)/shard_map/last_kernel/pallas_call | solution.py:495

commit v3 on v2

--- a/solution.py
+++ b/solution.py
@@ -131,6 +131,20 @@
 
 
 FORWARD_PLAN = (
+    (2, "pair_totals", 0),
+    (3, "pair_totals", 1),
+    (5, "pair_totals", 2),
+    (6, "pair_totals", 3),
+    (6, "row_totals", 0),
+    (7, "row_totals", 1),
+    (9, "row_totals", 2),
+    (10, "row_totals", 3),
+    (10, "edges", 0),
+    (11, "edges", 1),
+    (13, "edges", 2),
+    (14, "edges", 3),
+)
+BACKWARD_PLAN = (
     (1, "pair_totals", 0),
     (2, "pair_totals", 1),
     (3, "pair_totals", 2),
@@ -138,27 +152,20 @@
     (4, "row_totals", 0),
     (5, "row_totals", 1),
     (6, "row_totals", 2),
-)
-BACKWARD_PLAN = (
-    (0, "pair_totals", 0),
-    (1, "pair_totals", 1),
-    (2, "pair_totals", 2),
-    (3, "pair_totals", 3),
-    (3, "row_totals", 0),
-    (4, "row_totals", 1),
-    (4, "row_totals", 2),
-    (5, "row_totals", 3),
-    (5, "edges", 0),
-    (6, "edges", 1),
+    (8, "row_totals", 3),
+    (8, "edges", 0),
+    (9, "edges", 1),
+    (10, "edges", 2),
+    (11, "edges", 3),
 )
 
 
 def main_kernel(
     full_width,
-    lengths, rates, gain, queries, keys, values, out_grad,
+    lengths_in, rates_in, gain_in, queries, keys, values, out_grad,
     normed, grad_query, key_part, value_part, key_dev, value_dev, beyond,
-    query, key, value, cotangent, raw, scaled, weights, probs_t, query_in_t, query_dev, query_dev_t,
-    key_in, grad_raw, state_local, state_half_t, chain, inverse_at, pull_at,
+    lengths, rates, gain, query, key, value, cotangent, raw, scaled, weights, probs_t, query_in_t, query_dev, query_dev_t,
+    key_in, grad_raw, ahead, state_local, state_half_t, chain, inverse_at, pull_at,
     running, entering_gain, leaving_gain, keeping, before, after, documents,
     own_f, first_f, totals_f, mate_f, row_f, row_in_f, back_f, entering,
     own_b, first_b, totals_b, mate_b, row_b, row_in_b, back_b,
@@ -168,14 +175,27 @@
     value_in = cotangent
     x, z, head = lax.axis_index("x"), lax.axis_index("z"), lax.axis_index("head")
     me = x * 4 + z
+    half = HEADS // 2 * BLOCK
+    mine_first = jnp.where((z == 0) | (z == 3), 0, half)
+    first, second = (pl.ds(pl.multiple_of(at, half), half) for at in (half - mine_first, mine_first))
     loads = [
         pltpu.make_async_copy(source, target, load_sem.at[i])
         for i, (source, target) in enumerate(
-            ((keys, key), (values, value), (queries, query), (out_grad, cotangent))
+            (
+                (rates_in, rates),
+                (lengths_in, lengths),
+                (keys.at[:, first], key.at[:, first]),
+                (values.at[:, first], value.at[:, first]),
+                (keys.at[:, second], key.at[:, second]),
+                (values.at[:, second], value.at[:, second]),
+                (gain_in, gain),
+                (queries, query),
+                (out_grad, cotangent),
+            )
         )
     ]
-    loads[0].start()
-    loads[1].start()
+    for load in loads[:6]:
+        load.start()
     barrier = pltpu.get_barrier_semaphore()
     peers = [(x, z + 1 - 2 * lax.rem(z, 2), head), (x, 3 - z, head)]
     peers += [(lax.rem(x + step, 4), z, head) for step in (1, 3)]
@@ -183,6 +203,8 @@
     for peer in peers:
         pl.semaphore_signal(barrier, inc=1, device_id=peer, device_id_type=MESH)
 
+    loads[0].wait()
+    loads[1].wait()
     lane = lax.broadcasted_iota(jnp.int32, (BLOCK, BLOCK), 1)
     sublane = lax.broadcasted_iota(jnp.int32, (BLOCK, BLOCK), 0)
     upto = (sublane <= lane).astype(F32).astype(BF16)
@@ -235,11 +257,14 @@
     forward.prepare()
     backward.prepare()
 
-    loads[0].wait()
-    loads[1].wait()
-    loads[2].start()
-    loads[3].start()
+    loads[2].wait()
+    loads[3].wait()
     for turn, h in enumerate(forward.other + forward.mine):
+        if turn == 4:
+            for load in loads[4:6]:
+                load.wait()
+            for load in loads[6:]:
+                load.start()
         lanes = rows_of(h)
         pieces = []
         for b in range(BLOCKS):
@@ -251,49 +276,69 @@
         if turn < 4:
             forward.start(turn)
     chain[...] = jnp.zeros_like(chain)
-    loads[2].wait()
-    loads[3].wait()
-
-    def local(b, carry):
+    for load in loads[6:]:
+        load.wait()
+
+    last_step = 2 * BLOCKS - 1
+
+    def local_scores(step):
+        b, group = lax.div(step, 2), lax.rem(step, 2)
         rows = rows_of(b)
         doc_row = documents[pl.ds(b, 1), :]
         same = (sublane >= lane) & (as_columns(doc_row) == jnp.broadcast_to(doc_row, (BLOCK, BLOCK)))
         bias = jnp.where(same, 0.0, MASKED)
-        for h in range(HEADS):
-            lanes = static_rows(h)
+        for j in range(HEADS // 2):
+            h = group * (HEADS // 2) + j
+            lanes = rows_of(h)
             query_b, key_b, value_b = query[rows, lanes], key[rows, lanes], value[rows, lanes]
-            run_row = running[b, h : h + 1]
+            run_row = running[b, pl.ds(h, 1)]
             weight = jnp.exp(as_columns(run_row) - run_row + bias)
             weights[b, h] = weight
             probs = (dot(query_b, key_b, 1, 1) * weight).astype(BF16)
+            ahead[0, j] = probs
             probs_t[b, h] = jnp.transpose(probs)
-            query_e = query_b.astype(F32) * as_columns(entering_gain[b, h : h + 1])
+            query_e = query_b.astype(F32) * as_columns(entering_gain[b, pl.ds(h, 1)])
             query_in = query_e.astype(BF16)
+            ahead[1, j] = query_in
             query_in_t[b, h] = jnp.transpose(query_in)
-            query_d = (query_e * before[b, h : h + 1]).astype(BF16)
+            query_d = (query_e * before[b, pl.ds(h, 1)]).astype(BF16)
             query_dev[rows, lanes] = query_d
             query_dev_t[h, :, rows] = jnp.transpose(query_d)
-            leave = as_columns(leaving_gain[b, h : h + 1])
-            after_row = after[b, h : h + 1]
+            leave = as_columns(leaving_gain[b, pl.ds(h, 1)])
+            after_row = after[b, pl.ds(h, 1)]
             key_l = key_b.astype(F32) * leave
             key_lb = key_l.astype(BF16)
             key_in[rows, lanes] = key_lb
+            ahead[2, j] = jnp.transpose(key_lb)
             key_dev[rows, lanes] = (key_l * after_row).astype(BF16)
             scaled[rows, lanes] = cotangent[rows, lanes].astype(F32) * gain[:, lanes]
             value_l = value_b.astype(F32) * leave
             value_in[rows, lanes] = value_l.astype(BF16)
             value_dev[rows, lanes] = (value_l * after_row).astype(BF16)
+
+    def local(step):
+        b, group = lax.div(step, 2), lax.rem(step, 2)
+        rows = rows_of(b)
+        for j in range(HEADS // 2):
+            h = group * (HEADS // 2) + j
+            lanes = rows_of(h)
+            value_b = value[rows, lanes]
             state = chain[h]
             state_local[b, h] = state
             raw[rows, lanes] = dot(
-                jnp.concatenate([probs, query_in], axis=1), jnp.concatenate([value_b, state.astype(BF16)])
+                jnp.concatenate([ahead[0, j], ahead[1, j]], axis=1), jnp.concatenate([value_b, state.astype(BF16)])
             )
-            chain[h] = keeping[b, h : h + 1] * state + dot(jnp.transpose(key_lb), value_b)
-        forward.serve(b, FORWARD_PLAN)
+            chain[h] = keeping[b, pl.ds(h, 1)] * state + dot(ahead[2, j], value_b)
+
+    def local_step(step, carry):
+        local(step)
+        local_scores(step + 1)
+        forward.serve(step, FORWARD_PLAN)
         return carry
 
-    lax.fori_loop(0, BLOCKS, local, 0)
-    forward.row_totals(3)
+    local_scores(jnp.int32(0))
+    lax.fori_loop(0, last_step, local_step, 0)
+    local(jnp.int32(last_step))
     squares, projected = inverse_at, pull_at
     squares[...] = jnp.zeros_like(squares)
     projected[...] = jnp.zeros_like(projected)
@@ -309,7 +354,6 @@
             projected[b] += out * scaled[rows, lanes]
 
     for k in range(4):
-        forward.edges(k)
         finish_raw(forward.mine[k])
     for k in range(4):
         forward.arrive(k)
@@ -363,36 +407,51 @@
     for j in range(7):
         shares[j].wait_send()
 
-    def gradients(step, carry):
-        b = BLOCKS - 1 - step
+    def gradient_scores(step):
+        b, group = BLOCKS - 1 - lax.div(step, 2), lax.rem(step, 2)
         rows = rows_of(b)
-        for h in range(HEADS):
-            lanes = static_rows(h)
+        for j in range(HEADS // 2):
+            h = group * (HEADS // 2) + j
+            lanes = rows_of(h)
             grad = grad_raw[rows, lanes]
             mixed = (dot(grad, value[rows, lanes], 1, 1) * weights[b, h]).astype(BF16)
-            grad_in = (grad.astype(F32) * as_columns(entering_gain[b, h : h + 1])).astype(BF16)
+            ahead[0, j] = mixed
+            ahead[1, j] = jnp.transpose(mixed)
+            ahead[2, j] = (grad.astype(F32) * as_columns(entering_gain[b, pl.ds(h, 1)])).astype(BF16)
+
+    def gradients(step):
+        b, group = BLOCKS - 1 - lax.div(step, 2), lax.rem(step, 2)
+        rows = rows_of(b)
+        for j in range(HEADS // 2):
+            h = group * (HEADS // 2) + j
+            lanes = rows_of(h)
+            grad = grad_raw[rows, lanes]
             grad_query[rows, lanes] = dot(
-                jnp.concatenate([mixed, grad_in], axis=1),
+                jnp.concatenate([ahead[0, j], ahead[2, j]], axis=1),
                 jnp.concatenate([key[rows, lanes], state_half_t[b, h]]),
             ).astype(BF16)
             carried = chain[h]
             carried_half = carried.astype(BF16)
             key_part[rows, lanes] = dot(
-                jnp.concatenate([jnp.transpose(mixed), value_in[rows, lanes]], axis=1),
+                jnp.concatenate([ahead[1, j], value_in[rows, lanes]], axis=1),
                 jnp.concatenate([query[rows, lanes], jnp.transpose(carried_half)]),
             )
             value_part[rows, lanes] = dot(
                 jnp.concatenate([probs_t[b, h], key_in[rows, lanes]], axis=1),
                 jnp.concatenate([grad, carried_half]),
             )
-            chain[h] = keeping[b, h : h + 1] * carried + dot(query_in_t[b, h], grad)
+            chain[h] = keeping[b, pl.ds(h, 1)] * carried + dot(query_in_t[b, h], grad)
             normed[rows, lanes] = (raw[rows, lanes] * inverse_at[b] * gain[:, lanes]).astype(BF16)
+
+    def gradient_step(step, carry):
+        gradients(step)
+        gradient_scores(step + 1)
         backward.serve(step, BACKWARD_PLAN)
         return carry
 
-    lax.fori_loop(0, BLOCKS, gradients, 0)
-    backward.edges(2)
-    backward.edges(3)
+    gradient_scores(jnp.int32(0))
+    lax.fori_loop(0, last_step, gradient_step, 0)
+    gradients(jnp.int32(last_step))
     for k in range(4):
         backward.arrive(k)
     backward.finish()
@@ -401,7 +460,7 @@
 def last_kernel(
     normed_in, query_in, key_part, value_part, key_dev, value_dev, beyond,
     normed, grad_query, grad_key, grad_value,
-    key_rows, value_rows, pass_sem, key_sem, value_sem,
+    key_rows, value_rows, plain, turned, pass_sem, key_sem, value_sem,
 ):
     passes = [
         pltpu.make_async_copy(normed_in, normed, pass_sem.at[0]),
@@ -410,25 +469,33 @@
     for copy in passes:
         copy.start()
 
+    tall = 2 * BLOCK
+
     def stores(b):
-        rows = rows_of(b)
+        rows = pl.ds(pl.multiple_of(b * tall, tall), tall)
         return (
             pltpu.make_async_copy(key_rows.at[rows], grad_key.at[rows], key_sem.at[b]),
             pltpu.make_async_copy(value_rows.at[rows], grad_value.at[rows], value_sem.at[b]),
         )
 
+    zero = jnp.zeros((BLOCK, BLOCK), BF16)
+    for h in range(HEADS):
+        state = beyond[h].astype(BF16)
+        for states, part in ((plain, state), (turned, jnp.transpose(state))):
+            pair = (part, zero) if h % 2 == 0 else (zero, part)
+            states[h // 2, static_rows(h % 2)] = jnp.concatenate(pair, axis=1)
+
     def block(b, carry):
-        rows = rows_of(b)
-        for h in range(HEADS):
-            lanes = static_rows(h)
-            carried = beyond[h].astype(BF16)
-            key_rows[rows, lanes] = (key_part[rows, lanes] + dot(value_dev[rows, lanes], carried, 1, 1)).astype(BF16)
-            value_rows[rows, lanes] = (value_part[rows, lanes] + dot(key_dev[rows, lanes], carried)).astype(BF16)
+        rows = pl.ds(pl.multiple_of(b * tall, tall), tall)
+        for pair in range(HEADS // 2):
+            lanes = slice(pair * tall, (pair + 1) * tall)
+            key_rows[rows, lanes] = (key_part[rows, lanes] + dot(value_dev[rows, lanes], turned[pair])).astype(BF16)
+            value_rows[rows, lanes] = (value_part[rows, lanes] + dot(key_dev[rows, lanes], plain[pair])).astype(BF16)
         for copy in stores(b):
             copy.start()
         return carry
 
-    lax.fori_loop(0, BLOCKS, block, 0)
+    lax.fori_loop(0, BLOCKS // 2, block, 0)
     for copy in passes:
         copy.wait()
 
@@ -437,7 +504,7 @@
             copy.wait()
         return carry
 
-    lax.fori_loop(0, BLOCKS, settle, 0)
+    lax.fori_loop(0, BLOCKS // 2, settle, 0)
 
 
 def body(queries, keys, values, log_decay, gain, lengths, out_grad):
@@ -455,13 +522,17 @@
     wires = [own, slab, slab, slab, part, part, part]
     half, full = pltpu.VMEM(wide, BF16), pltpu.VMEM(wide, F32)
     handed = (half, half, full, full, half, half, states)
+    two_heads = pltpu.VMEM((HEADS // 2, 2 * BLOCK, 2 * BLOCK), BF16)
     dma = pltpu.SemaphoreType.DMA
     found = pl.pallas_call(
         functools.partial(main_kernel, full_width),
         out_shape=handed,
-        in_specs=[pl.BlockSpec(memory_space=pltpu.SMEM), vmem, vmem, hbm, hbm, hbm, hbm],
+        in_specs=[hbm] * 7,
         out_specs=(vmem,) * len(handed),
         scratch_shapes=[
+            pltpu.SMEM((8,), jnp.int32),
+            pltpu.VMEM((HEADS, rows), F32),
+            pltpu.VMEM((1, width), F32),
             half, half, half, half, full, full,
             pltpu.VMEM(tiles, F32),
             pltpu.VMEM(tiles, BF16),
@@ -469,6 +540,7 @@
             half,
             pltpu.VMEM((HEADS, BLOCK, rows), BF16),
             half, half,
+            pltpu.VMEM((3, HEADS // 2, BLOCK, BLOCK), BF16),
             pltpu.VMEM(tiles, F32),
             pltpu.VMEM(tiles, BF16),
             states, states, states,
@@ -479,7 +551,7 @@
             *wires,
             pltpu.VMEM((2, BLOCKS, BLOCK), F32),
             pltpu.VMEM((7, 2, BLOCKS, BLOCK), F32),
-            dma((4,)),
+            dma((9,)),
             dma((16,)),
             dma((16,)),
             dma((16,)),
@@ -497,7 +569,7 @@
         out_shape=(jax.ShapeDtypeStruct(wide, BF16),) * 4,
         in_specs=[vmem] * len(handed),
         out_specs=(hbm,) * 4,
-        scratch_shapes=[half, half, dma((2,)), dma((8,)), dma((8,))],
+        scratch_shapes=[half, half, two_heads, two_heads, dma((2,)), dma((4,)), dma((4,))],
         compiler_params=pltpu.CompilerParams(vmem_limit_bytes=8 * 2**20),
         name="last_kernel",
     )(*found)

time: 59.9 us -> 57.6 us (0.962)
  Pallas kernels: 59.1 us -> 56.9 us
    pallas_call x1, Pallas kernels: 55.2 us -> 53.5 us  [body(): pl.pallas_call(functools.partial(main_kernel, full_width), out_shape=hand...]
where the time goes in v3:
time: 57.6 us; the launch traced here: 57.5 us
  Pallas kernels  56.9 us (99%)
  between operations  0.64 us (1%)
    pallas_call x1, Pallas kernels, body(): pl.pallas_call(functools.partial(main_kernel, full_width), out_shape=hand...  53.5 us
    pallas_call x1, Pallas kernels, body(): pl.pallas_call(last_kernel, out_shape=(jax.ShapeDtypeStruct(wide, BF16),)...  3.37 us

profile of v3, /device:TPU:0, one launch (start us, length us, event | category | flops | bytes accessed | tf_op | source)
XLA Modules:
  0.0 57.5 jit_solution(12343610052741277189)
XLA Ops:
  0.6 53.5 %main_kernel.1 = (bf16[1024,1024]{1,0:T(8,128)(2,1)S(1)}, bf16[1024,1024]{1,0:T(8,128)(2,1)S(1)}, f32[1024,1024]{1,0:T(8,128)S(1)}, f32[1024,1024]{1,0:T(8,128)S...) custom-call(s32[8]{0:T(128)} %lengths_in.1, f32[8,1024]{1,0:T(8,128)} %bitcast.2, ...), custom_call_target="tpu_custom_call" | custom-call | tf_op jit(solution)/shard_map/main_kernel/pallas_call | solution.py:527
  54.2 3.4 %last_kernel.1 = (bf16[1024,1024]{1,0:T(8,128)(2,1)}, bf16[1024,1024]{1,0:T(8,128)(2,1)}, bf16[1024,1024]{1,0:T(8,128)(2,1)}, bf16[1024,1024]{1,0:T(8,128)(2,1)}) custom-call(bf16[1024,1024]{1,0:T(8,128)(2,1)S(1)} %get-tuple-element.11.normed_in, bf16[1024,1024]{1,0:T(8,128)(2,1)S(1)} %get-tuple-element.12.query_in, ...), custom_call_target="tpu_custom_call" | custom-call | tf_op jit(solution)/shard_map/last_kernel/pallas_call | solution.py:567

commit v4 on v3

--- a/solution.py
+++ b/solution.py
@@ -131,24 +131,10 @@
 
 
 FORWARD_PLAN = (
-    (2, "pair_totals", 0),
-    (3, "pair_totals", 1),
-    (5, "pair_totals", 2),
-    (6, "pair_totals", 3),
-    (6, "row_totals", 0),
-    (7, "row_totals", 1),
-    (9, "row_totals", 2),
-    (10, "row_totals", 3),
-    (10, "edges", 0),
-    (11, "edges", 1),
-    (13, "edges", 2),
-    (14, "edges", 3),
-)
-BACKWARD_PLAN = (
-    (1, "pair_totals", 0),
-    (2, "pair_totals", 1),
-    (3, "pair_totals", 2),
-    (4, "pair_totals", 3),
+    (0, "pair_totals", 0),
+    (1, "pair_totals", 1),
+    (2, "pair_totals", 2),
+    (3, "pair_totals", 3),
     (4, "row_totals", 0),
     (5, "row_totals", 1),
     (6, "row_totals", 2),
@@ -156,7 +142,21 @@
     (8, "edges", 0),
     (9, "edges", 1),
     (10, "edges", 2),
-    (11, "edges", 3),
+    (12, "edges", 3),
+)
+BACKWARD_PLAN = (
+    (0, "pair_totals", 0),
+    (1, "pair_totals", 1),
+    (2, "pair_totals", 2),
+    (4, "pair_totals", 3),
+    (4, "row_totals", 0),
+    (5, "row_totals", 1),
+    (6, "row_totals", 2),
+    (7, "row_totals", 3),
+    (7, "edges", 0),
+    (8, "edges", 1),
+    (9, "edges", 2),
+    (10, "edges", 3),
 )
 
 

time: 57.6 us -> 56.4 us (0.979)
  Pallas kernels: 56.9 us -> 55.6 us
    pallas_call x1, Pallas kernels: 53.5 us -> 52.3 us  [body(): pl.pallas_call(functools.partial(main_kernel, full_width), out_shape=hand...]
where the time goes in v4:
time: 56.4 us; the launch traced here: 56.3 us
  Pallas kernels  55.6 us (99%)
  between operations  0.64 us (1%)
    pallas_call x1, Pallas kernels, body(): pl.pallas_call(functools.partial(main_kernel, full_width), out_shape=hand...  52.3 us
    pallas_call x1, Pallas kernels, body(): pl.pallas_call(last_kernel, out_shape=(jax.ShapeDtypeStruct(wide, BF16),)...  3.37 us

profile of v4, /device:TPU:0, one launch (start us, length us, event | category | flops | bytes accessed | tf_op | source)
XLA Modules:
  0.0 56.3 jit_solution(6140148001785202369)
XLA Ops:
  0.6 52.3 %main_kernel.1 = (bf16[1024,1024]{1,0:T(8,128)(2,1)S(1)}, bf16[1024,1024]{1,0:T(8,128)(2,1)S(1)}, f32[1024,1024]{1,0:T(8,128)S(1)}, f32[1024,1024]{1,0:T(8,128)S...) custom-call(s32[8]{0:T(128)} %lengths_in.1, f32[8,1024]{1,0:T(8,128)} %bitcast.2, ...), custom_call_target="tpu_custom_call" | custom-call | tf_op jit(solution)/shard_map/main_kernel/pallas_call | solution.py:527
  52.9 3.4 %last_kernel.1 = (bf16[1024,1024]{1,0:T(8,128)(2,1)}, bf16[1024,1024]{1,0:T(8,128)(2,1)}, bf16[1024,1024]{1,0:T(8,128)(2,1)}, bf16[1024,1024]{1,0:T(8,128)(2,1)}) custom-call(bf16[1024,1024]{1,0:T(8,128)(2,1)S(1)} %get-tuple-element.11.normed_in, bf16[1024,1024]{1,0:T(8,128)(2,1)S(1)} %get-tuple-element.12.query_in, ...), custom_call_target="tpu_custom_call" | custom-call | tf_op jit(solution)/shard_map/last_kernel/pallas_call | solution.py:567

commit v5 on v4

--- a/solution.py
+++ b/solution.py
@@ -259,12 +259,12 @@
 
     loads[2].wait()
     loads[3].wait()
+    for load in loads[6:]:
+        load.start()
     for turn, h in enumerate(forward.other + forward.mine):
         if turn == 4:
             for load in loads[4:6]:
                 load.wait()
-            for load in loads[6:]:
-                load.start()
         lanes = rows_of(h)
         pieces = []
         for b in range(BLOCKS):

time: 56.4 us -> 54.6 us (0.968)
  Pallas kernels: 55.6 us -> 53.9 us
    pallas_call x1, Pallas kernels: 52.3 us -> 50.5 us  [body(): pl.pallas_call(functools.partial(main_kernel, full_width), out_shape=hand...]
where the time goes in v5:
time: 54.6 us; the launch traced here: 54.5 us
  Pallas kernels  53.9 us (99%)
  between operations  0.64 us (1%)
    pallas_call x1, Pallas kernels, body(): pl.pallas_call(functools.partial(main_kernel, full_width), out_shape=hand...  50.5 us
    pallas_call x1, Pallas kernels, body(): pl.pallas_call(last_kernel, out_shape=(jax.ShapeDtypeStruct(wide, BF16),)...  3.37 us

profile of v5, /device:TPU:0, one launch (start us, length us, event | category | flops | bytes accessed | tf_op | source)
XLA Modules:
  0.0 54.5 jit_solution(13243205191062613311)
XLA Ops:
  0.6 50.5 %main_kernel.1 = (bf16[1024,1024]{1,0:T(8,128)(2,1)S(1)}, bf16[1024,1024]{1,0:T(8,128)(2,1)S(1)}, f32[1024,1024]{1,0:T(8,128)S(1)}, f32[1024,1024]{1,0:T(8,128)S...) custom-call(s32[8]{0:T(128)} %lengths_in.1, f32[8,1024]{1,0:T(8,128)} %bitcast.2, ...), custom_call_target="tpu_custom_call" | custom-call | tf_op jit(solution)/shard_map/main_kernel/pallas_call | solution.py:527
  51.1 3.4 %last_kernel.1 = (bf16[1024,1024]{1,0:T(8,128)(2,1)}, bf16[1024,1024]{1,0:T(8,128)(2,1)}, bf16[1024,1024]{1,0:T(8,128)(2,1)}, bf16[1024,1024]{1,0:T(8,128)(2,1)}) custom-call(bf16[1024,1024]{1,0:T(8,128)(2,1)S(1)} %get-tuple-element.11.normed_in, bf16[1024,1024]{1,0:T(8,128)(2,1)S(1)} %get-tuple-element.12.query_in, ...), custom_call_target="tpu_custom_call" | custom-call | tf_op jit(solution)/shard_map/last_kernel/pallas_call | solution.py:567
